TPU v7x, 32 devices: a whole 2x2x4 slice. The times are simulated.
32 devices in a mesh: chain: 8 (over y, x, core), col: 4 (over z).
Axes of the slice: x: 2, y: 2, z: 4, core: 2. Of those that a mesh axis runs over, the one named last changes fastest.
Arguments:
- rhs: bfloat16 [16, 64, 2560], P('chain', None, 'col'), may hold values from -6 to 6
- block_inverse: bfloat16 [16, 2560, 2560], P('chain', 'col'), as said below
- entry_factor: bfloat16 [16, 2560, 128], P('chain', 'col'), as said below
- exit_factor: bfloat16 [16, 2560, 128], P('chain', 'col'), as said below
- previous: bfloat16 [64, 2560], P(None, 'col'), may hold values from -6 to 6
Outputs:
- solution: float32 [16, 64, 2560], P('chain', None, 'col')
Inputs may be any that keep to these rules, and one draw needn't show every extreme that they name: Every block of block_inverse equals its own transpose. `entry_factor`: entries are independent, of mean zero. `exit_factor`: entries are independent, of mean zero.
All inputs are finite; a program needn't handle non-finite values.
Results may differ from a plain program's by a relative error of at most 0.0003.
Values may be sent and summed in bfloat16 or wider, within the bound.
A program may use at most 64 MiB of HBM per device.

v0:
```python
import jax
import jax.numpy as jnp
from jax import lax
from jax.sharding import PartitionSpec as P


def from_behind(block, axis, distance):
    devices = range(lax.axis_size(axis))
    route = [(i - distance, i) for i in devices if i - distance in devices]
    return lax.ppermute(block, axis, route)


def entering(part, axis, combine, identity, reverse):
    count = lax.axis_size(axis)
    place = lax.axis_index(axis)
    ahead = count - 1 - place if reverse else place
    gathered = jax.tree.map(lambda a: lax.all_gather(a, axis), part)
    state = jax.tree.map(lambda a, e: jnp.zeros_like(a) + jnp.asarray(e, a.dtype), part, identity)

    def one(step, state):
        source = count - 1 - step if reverse else step
        return combine(
            state, jax.tree.map(lambda a: lax.dynamic_index_in_dim(a, source, 0, False), gathered)
        )

    return lax.fori_loop(0, ahead, one, state)


def compose(earlier, later):
    exact = lax.Precision.HIGHEST
    first_map, first_shift = earlier
    second_map, second_shift = later
    return (
        jnp.dot(first_map, second_map, precision=exact),
        jnp.dot(first_shift, second_map, precision=exact) + second_shift,
    )


def shards(rhs, block_inverse, entry_factor, exit_factor, previous):
    exact = lax.Precision.HIGHEST
    intervals_here = rhs.shape[0]
    column_count = rhs.shape[1]
    state_width = entry_factor.shape[2]
    arriving = from_behind(exit_factor[:1], "chain", -1)
    following = jnp.concatenate([exit_factor[1:], arriving], axis=0)
    couple_part = -jnp.einsum(
        "irn,irm->inm", entry_factor, following, preferred_element_type=jnp.float32
    )
    source_part = jnp.einsum("icr,irm->icm", rhs, following, preferred_element_type=jnp.float32)
    opening_part = jnp.dot(previous, exit_factor[0], preferred_element_type=jnp.float32)
    couple, source, opening = lax.psum((couple_part, source_part, opening_part), "col")
    identity = jnp.eye(state_width, dtype=jnp.float32)
    empty_shift = jnp.zeros((column_count, state_width), jnp.float32)
    first_chain = lax.axis_index("chain") == 0
    matrix = identity
    offset = empty_shift
    for position in range(intervals_here):
        matrix = jnp.dot(matrix, couple[position], precision=exact)
        offset = jnp.dot(offset, couple[position], precision=exact) + source[position]
    folded = jnp.dot(opening, matrix, precision=exact) + offset
    offset = jnp.where(first_chain, folded, offset)
    matrix = jnp.where(first_chain, jnp.zeros_like(matrix), matrix)
    _, incoming = entering((matrix, offset), "chain", compose, (identity, empty_shift), False)
    carry_state = jnp.where(first_chain, opening, incoming)
    solved_list = []
    for position in range(intervals_here):
        solved_list.append(
            rhs[position].astype(jnp.float32)
            - jnp.dot(carry_state, entry_factor[position].astype(jnp.float32).T, precision=exact)
        )
        carry_state = jnp.dot(carry_state, couple[position], precision=exact) + source[position]
    forward = jnp.stack(solved_list).astype(jnp.bfloat16)
    applied = jnp.einsum(
        "icb,irb->icr",
        lax.all_gather(forward, "col", axis=2, tiled=True),
        block_inverse,
        preferred_element_type=jnp.float32,
    )
    carried_part = jnp.einsum(
        "icr,irn->icn",
        applied.astype(jnp.bfloat16),
        entry_factor,
        preferred_element_type=jnp.float32,
    )
    carried = lax.psum(carried_part, "col")
    last_chain = lax.axis_index("chain") == lax.axis_size("chain") - 1
    matrix = identity
    offset = empty_shift
    for position in reversed(range(intervals_here)):
        turned = couple[position].T
        matrix = jnp.dot(matrix, turned, precision=exact)
        offset = jnp.dot(offset, turned, precision=exact) + carried[position]
    matrix = jnp.where(last_chain, jnp.zeros_like(matrix), matrix)
    _, behind = entering((matrix, offset), "chain", compose, (identity, empty_shift), True)
    results = [None] * intervals_here
    for position in reversed(range(intervals_here)):
        results[position] = applied[position] - jnp.dot(
            behind, following[position].astype(jnp.float32).T, precision=exact
        )
        behind = jnp.dot(behind, couple[position].T, precision=exact) + carried[position]
    return jnp.stack(results)


def solution(mesh):
    placed = (
        P("chain", None, "col"),
        P("chain", "col", None),
        P("chain", "col", None),
        P("chain", "col", None),
        P(None, "col"),
    )
    return jax.shard_map(
        shards, mesh=mesh, in_specs=placed, out_specs=P("chain", None, "col"), check_vma=False
    )
```

profile of v0, /device:TPU:0, one launch (start us, length us, event | category | flops | bytes accessed | tf_op | source)
XLA Modules:
  0.0 161.5 jit_solution(1179635024437629665)
XLA Ops:
  6.5 1.1 fusion.37
  7.8 1.3 collective-permute-start
  9.3 1.8 %collective-permute-done = bf16[1,640,128]{1,2,0:T(8,128)(2,1)S(1)} collective-permute-done((bf16[1,640,128]{1,2,0:T(8,128)(2,1)S(1)}, bf16[1,640,128]{1,2,0:T(8,128)(2,1)S(1)}, u32[]{:S(2)}, u32[]{:S(2)}) %collective-permute-start) | collective-permute-done | bytes 163872 | tf_op jit(solution)/shard_map/ppermute | solution.py:10
  11.1 1.8 %convolution_bitcast_fusion.2 = f32[2,64,128]{2,1,0:T(8,128)} fusion(bf16[2,64,640]{2,1,0:T(8,128)(2,1)} %param.9, bf16[1,640,128]{1,2,0:T(8,128)(2,1)S(1)} %collective-permute-done, bf16[1,640,128]{1,2,0:T(8,128)(2,1)S(1)} %copy.11), kind=kOutput, calls=%fused_computation.23 | convolution fusion | flops 21135360 | bytes 557056 | tf_op jit(solution)/shard_map/icr,irm->icm/dot_general | solution.py:49
  12.9 1.9 %fusion.10 = f32[2,128,128]{1,2,0:T(8,128)} fusion(bf16[2,640,128]{2,1,0:T(8,128)(2,1)} %param.11, bf16[1,640,128]{1,2,0:T(8,128)(2,1)S(1)} %collective-permute-done, bf16[1,640,128]{1,2,0:T(8,128)(2,1)S(1)} %copy.11), kind=kOutput, calls=%fused_computation.17 | convolution fusion | flops 42139648 | bytes 786432 | tf_op jit(solution)/shard_map/irn,irm->inm/dot_general | solution.py:46
  14.8 1.1 fusion.17
  15.9 21.0 %psum.28 = f32[64,128]{1,0:T(8,128)S(1)} all-reduce(f32[64,128]{1,0:T(8,128)S(1)} %fusion.17), channel_id=1, replica_groups=mesh['chain'=8,'col'=4] {'col'}, use_global_device_ids=true, to_apply=%region_0.0 | all-reduce | flops 8192 | bytes 65536 | tf_op jit(solution)/shard_map/psum | solution.py:51
  36.9 18.5 %all-reduce.6.cloned.1.call-done = (f32[2,128,128]{1,2,0:T(8,128)}, f32[2,64,128]{2,1,0:T(8,128)}) async-done(((f32[2,128,128]{1,2,0:T(8,128)}, f32[2,64,128]{2,1,0:T(8,128)}), (f32[2,128,128]{1,2,0:T(8,128)}, f32[2,64,128]{2,1,0:T(8,128)})) %all-reduce.6.cloned.1.call-update) | async-done | bytes 196624 | tf_op jit(solution)/shard_map/psum | solution.py:51
  55.4 1.1 fusion.27
  56.5 1.1 convolution_add_fusion.5
  57.6 1.1 convolution_add_fusion.4
  58.7 1.1 broadcast_select_fusion
  60.0 9.2 %all-gather.1 = f32[512,128]{1,0:T(8,128)S(1)} all-gather(f32[64,128]{1,0:T(8,128)S(1)} %fusion.15), channel_id=3, replica_groups=mesh['chain'=8,'col'=4] {'chain'}, dimensions={0}, use_global_device_ids=true | all-gather | bytes 294912 | tf_op jit(solution)/shard_map/all_gather | solution.py:17
  69.2 9.8 %all-gather = f32[1024,128]{1,0:T(8,128)S(1)} all-gather(f32[128,128]{1,0:T(8,128)S(1)} %get-tuple-element.159), channel_id=2, replica_groups=mesh['chain'=8,'col'=4] {'chain'}, dimensions={0}, use_global_device_ids=true | all-gather | bytes 589824 | tf_op jit(solution)/shard_map/all_gather | solution.py:17
  79.3 1.1 convolution_add_fusion.3
  80.5 1.0 fusion.26
  81.9 17.2 %all_gather.31 = bf16[2,64,2560]{2,1,0:T(8,128)(2,1)S(1)} all-gather(bf16[2,64,640]{2,1,0:T(8,128)(2,1)S(1)} %pad_maximum_fusion.4), channel_id=1, replica_groups=mesh['chain'=8,'col'=4] {'col'}, dimensions={2}, use_global_device_ids=true | all-gather | bytes 819200 | tf_op jit(solution)/shard_map/all_gather | solution.py:75
  99.1 4.9 %fusion.38 = f32[2,64,640]{2,1,0:T(8,128)S(1)} fusion(bf16[2,64,2560]{2,1,0:T(8,128)(2,1)S(1)} %all_gather.31, bf16[2,640,2560]{2,1,0:T(8,128)(2,1)} %param.10), kind=kOutput, calls=%fused_computation.68 | convolution fusion | flops 419430400 | bytes 7536640 | tf_op jit(solution)/shard_map/icb,irb->icr/dot_general | solution.py:73
  105.1 9.9 %all-gather.2 = f32[1024,128]{1,0:T(8,128)S(1)} all-gather(f32[128,128]{1,0:T(8,128)S(1)} %convolution_select_fusion), channel_id=4, replica_groups=mesh['chain'=8,'col'=4] {'chain'}, dimensions={0}, use_global_device_ids=true | all-gather | bytes 589824 | tf_op jit(solution)/shard_map/all_gather | solution.py:17
  115.0 24.6 %all-reduce.4.cloned.1.call-done = f32[2,64,128]{2,1,0:T(8,128)} async-done(((f32[2,64,128]{2,1,0:T(8,128)}), f32[2,64,128]{2,1,0:T(8,128)}) %all-reduce.4.cloned.1.call-update) | async-done | bytes 65552 | tf_op jit(solution)/shard_map/psum | solution.py:85
  140.5 0.9 convolution_add_fusion.1
  141.5 9.3 %all-gather.3 = f32[512,128]{1,0:T(8,128)S(1)} all-gather(f32[64,128]{1,0:T(8,128)S(1)} %convolution_add_fusion.1), channel_id=5, replica_groups=mesh['chain'=8,'col'=4] {'chain'}, dimensions={0}, use_global_device_ids=true | all-gather | bytes 294912 | tf_op jit(solution)/shard_map/all_gather | solution.py:17
  150.8 1.6 %while.27 = (s32[]{:T(128)}, f32[64,128]{1,0:T(8,128)S(1)}, s32[]{:T(128)}, f32[8,128,128]{2,1,0:T(8,128)S(1)}, f32[8,64,128]{2,1,0:T(8,128)S(1)}, /*index=5*/s32[]{:T(128)}, s32[]{:T(128)}, s32[]{:T(128)}, s32[]{:T(128)}) while((s32[]{:T(128)}, f32[64,128]{1,0:T(8,128)S(1)}, s32[]{:T(128)}, f32[8,128,128]{2,1,0:T(8,128)S(1)}, ...), condition=%wide.region_7.8_spmd, body=%wide.region_6.7_spmd.sunk | while | flops 12591110 | bytes 230539 | solution.py:26
  152.4 0.9 convolution_add_fusion
  (43 shorter events, 5.9 us)
Async XLA Ops:
  6.5 8.3 %copy-start = (bf16[64,640]{1,0:T(8,128)(2,1)S(1)}, bf16[64,640]{1,0:T(8,128)(2,1)}, u32[]{:S(2)}) copy-start(bf16[64,640]{1,0:T(8,128)(2,1)} %param.13) | copy-start | bytes 245764
  6.5 72.5 %copy-start.4 = (bf16[2,64,640]{2,1,0:T(8,128)(2,1)S(1)}, bf16[2,64,640]{2,1,0:T(8,128)(2,1)}, u32[]{:S(2)}) copy-start(bf16[2,64,640]{2,1,0:T(8,128)(2,1)} %param.9) | copy-start | bytes 491524
  6.5 72.5 %copy-start.2 = (bf16[2,640,128]{2,1,0:T(8,128)(2,1)S(1)}, bf16[2,640,128]{2,1,0:T(8,128)(2,1)}, u32[]{:S(2)}) copy-start(bf16[2,640,128]{2,1,0:T(8,128)(2,1)} %param.11) | copy-start | bytes 983044
  6.5 48.9 %all-reduce.6.cloned.1.call-start = ((), (), s32[]{:S(2)}) async-start(), calls=%async_computation.1 | async-start | bytes 393216 | tf_op jit(solution)/shard_map/psum | solution.py:51
  7.8 3.3 %collective-permute-start = (bf16[1,640,128]{1,2,0:T(8,128)(2,1)S(1)}, bf16[1,640,128]{1,2,0:T(8,128)(2,1)S(1)}, u32[]{:S(2)}, u32[]{:S(2)}) collective-permute-start(bf16[1,640,128]{1,2,0:T(8,128)(2,1)S(1)} %copy.10), channel_id=1, source_target_pairs={{4,0},{8,4},{12,8},{16,12},{20,16},{24,20},{28,24},{5,1},{9,5},{13... | collective-permute-start | bytes 491528 | tf_op jit(solution)/shard_map/ppermute | solution.py:10
  14.8 124.8 %all-reduce.4.cloned.1.call-start = ((), (), s32[]{:S(2)}) async-start(), calls=%async_computation | async-start | bytes 131072 | tf_op jit(solution)/shard_map/psum | solution.py:85
  59.8 45.1 %copy-start.1 = (f32[2,128,128]{1,2,0:T(8,128)S(1)}, f32[2,128,128]{1,2,0:T(8,128)}, u32[]{:S(2)}) copy-start(f32[2,128,128]{1,2,0:T(8,128)} %get-tuple-element.155) | copy-start | bytes 393220
  79.3 74.0 %copy-start.3 = (bf16[2,640,128]{2,1,0:T(8,128)(2,1)S(1)}, bf16[2,640,128]{2,1,0:T(8,128)(2,1)}, u32[]{:S(2)}) copy-start(bf16[2,640,128]{2,1,0:T(8,128)(2,1)} %param.12) | copy-start | bytes 983044
Sparse Core Ops, SparseCore 0:
  14.9 40.4 all-reduce.5
  105.0 34.5 all-reduce.3
where the time goes:
time: 162 us; the launch traced here: 161 us
  blocking collectives  76.4 us (47%)
  waiting for transfers between devices  45 us (28%)
  matrix products  22.7 us (14%)
  between operations  13.6 us (8%)
    all_gather x4, blocking collectives, entering(): gathered = jax.tree.map(lambda a: lax.all_gather(a, axis), part)  38.2 us
    psum x1, waiting for transfers between devices, shards(): carried = lax.psum(carried_part, 'col')  24.6 us
    psum x1, blocking collectives, shards(): lax.psum((couple_part, source_part, opening_part), 'col')  21 us
    psum x1, waiting for transfers between devices, shards(): lax.psum((couple_part, source_part, opening_part), 'col')  18.5 us
    all_gather x1, blocking collectives, shards(): lax.all_gather(forward, 'col', axis=2, tiled=True)  17.2 us
    dot_general x1, matrix products, shards(): jnp.einsum('icb,irb->icr', lax.all_gather(forward, 'col', axis=2, tiled=T...  4.94 us
  transfers between devices with their start and end apart: 3, of which 3 were waited for; matrix products, arithmetic and copies ran while one was open for 1% of the time, Pallas kernels for 0%

commit v1 on v0

--- a/solution.py
+++ b/solution.py
@@ -82,7 +82,7 @@
         entry_factor,
         preferred_element_type=jnp.float32,
     )
-    carried = lax.psum(carried_part, "col")
+    carried = jnp.sum(lax.all_gather(carried_part, "col"), axis=0)
     last_chain = lax.axis_index("chain") == lax.axis_size("chain") - 1
     matrix = identity
     offset = empty_shift

time: 162 us -> 149 us (0.920)
  waiting for transfers between devices: 45 us -> 20.5 us
  blocking collectives: 76.4 us -> 91.1 us
  matrix products: 22.7 us -> 19.8 us
    psum x1 -> x0, waiting for transfers between devices: 24.6 us -> none  [shards(): carried = lax.psum(carried_part, 'col')]
    all_gather x0 -> x1, blocking collectives: none -> 14.1 us  [shards(): carried = jnp.sum(lax.all_gather(carried_part, 'col'), axis=0)]
  transfers between devices with their start and end apart: 3 -> 2, of which waited for: 3 -> 2; matrix products, arithmetic and copies ran while one was open for 1% -> 1% of each run, Pallas kernels for 0% -> 0%
where the time goes in v1:
time: 149 us
  blocking collectives  91.1 us (61%)
  waiting for transfers between devices  20.5 us (14%)
  matrix products  19.8 us (13%)
  between operations  13.6 us (9%)
    all_gather x4, blocking collectives, entering(): gathered = jax.tree.map(lambda a: lax.all_gather(a, axis), part)  38.7 us
    psum x1, blocking collectives, shards(): lax.psum((couple_part, source_part, opening_part), 'col')  20.9 us
    psum x1, waiting for transfers between devices, shards(): lax.psum((couple_part, source_part, opening_part), 'col')  18.7 us
    all_gather x1, blocking collectives, shards(): lax.all_gather(forward, 'col', axis=2, tiled=True)  17.3 us
    all_gather x1, blocking collectives, shards(): carried = jnp.sum(lax.all_gather(carried_part, 'col'), axis=0)  14.1 us
    dot_general x1, matrix products, shards(): jnp.einsum('icb,irb->icr', lax.all_gather(forward, 'col', axis=2, tiled=T...  4.94 us
  transfers between devices with their start and end apart: 2, of which 2 were waited for; matrix products, arithmetic and copies ran while one was open for 1% of the time, Pallas kernels for 0%

profile of v1, /device:TPU:0, one launch (start us, length us, event | category | flops | bytes accessed | tf_op | source)
XLA Modules:
  0.0 148.7 jit_solution(4744948512112829492)
XLA Ops:
  6.5 1.1 fusion.37
  7.8 1.3 collective-permute-start
  9.3 1.8 %collective-permute-done = bf16[1,640,128]{1,2,0:T(8,128)(2,1)S(1)} collective-permute-done((bf16[1,640,128]{1,2,0:T(8,128)(2,1)S(1)}, bf16[1,640,128]{1,2,0:T(8,128)(2,1)S(1)}, u32[]{:S(2)}, u32[]{:S(2)}) %collective-permute-start) | collective-permute-done | bytes 163872 | tf_op jit(solution)/shard_map/ppermute | solution.py:10
  11.1 1.8 %convolution_bitcast_fusion.2 = f32[2,64,128]{2,1,0:T(8,128)} fusion(bf16[2,64,640]{2,1,0:T(8,128)(2,1)} %param.9, bf16[1,640,128]{1,2,0:T(8,128)(2,1)S(1)} %collective-permute-done, bf16[1,640,128]{1,2,0:T(8,128)(2,1)S(1)} %copy.14), kind=kOutput, calls=%fused_computation.23 | convolution fusion | flops 21135360 | bytes 557056 | tf_op jit(solution)/shard_map/icr,irm->icm/dot_general | solution.py:49
  12.9 1.9 %fusion.10 = f32[2,128,128]{1,2,0:T(8,128)} fusion(bf16[2,640,128]{2,1,0:T(8,128)(2,1)} %param.11, bf16[1,640,128]{1,2,0:T(8,128)(2,1)S(1)} %collective-permute-done, bf16[1,640,128]{1,2,0:T(8,128)(2,1)S(1)} %copy.14), kind=kOutput, calls=%fused_computation.17 | convolution fusion | flops 42139648 | bytes 786432 | tf_op jit(solution)/shard_map/irn,irm->inm/dot_general | solution.py:46
  14.8 1.1 fusion.17
  15.9 20.9 %psum.21 = f32[64,128]{1,0:T(8,128)S(1)} all-reduce(f32[64,128]{1,0:T(8,128)S(1)} %fusion.17), channel_id=1, replica_groups=mesh['chain'=8,'col'=4] {'col'}, use_global_device_ids=true, to_apply=%region_0.0 | all-reduce | flops 8192 | bytes 65536 | tf_op jit(solution)/shard_map/psum | solution.py:51
  36.8 18.7 %all-reduce.3.cloned.1.call-done = (f32[2,128,128]{1,2,0:T(8,128)}, f32[2,64,128]{2,1,0:T(8,128)}) async-done(((f32[2,128,128]{1,2,0:T(8,128)}, f32[2,64,128]{2,1,0:T(8,128)}), (f32[2,128,128]{1,2,0:T(8,128)}, f32[2,64,128]{2,1,0:T(8,128)})) %all-reduce.3.cloned.1.call-update) | async-done | bytes 196624 | tf_op jit(solution)/shard_map/psum | solution.py:51
  55.5 1.1 fusion.27
  56.5 1.1 convolution_add_fusion.5
  57.6 1.1 convolution_add_fusion.4
  58.7 1.1 broadcast_select_fusion
  60.0 9.2 %all-gather.1 = f32[512,128]{1,0:T(8,128)S(1)} all-gather(f32[64,128]{1,0:T(8,128)S(1)} %fusion.15), channel_id=3, replica_groups=mesh['chain'=8,'col'=4] {'chain'}, dimensions={0}, use_global_device_ids=true | all-gather | bytes 294912 | tf_op jit(solution)/shard_map/all_gather | solution.py:17
  69.2 9.9 %all-gather = f32[1024,128]{1,0:T(8,128)S(1)} all-gather(f32[128,128]{1,0:T(8,128)S(1)} %get-tuple-element.159), channel_id=2, replica_groups=mesh['chain'=8,'col'=4] {'chain'}, dimensions={0}, use_global_device_ids=true | all-gather | bytes 589824 | tf_op jit(solution)/shard_map/all_gather | solution.py:17
  79.2 0.3 fusion.14
  79.5 1.1 convolution_add_fusion.3
  80.6 1.0 fusion.26
  82.0 17.3 %all_gather.37 = bf16[2,64,2560]{2,1,0:T(8,128)(2,1)S(1)} all-gather(bf16[2,64,640]{2,1,0:T(8,128)(2,1)S(1)} %pad_maximum_fusion.4), channel_id=1, replica_groups=mesh['chain'=8,'col'=4] {'col'}, dimensions={2}, use_global_device_ids=true | all-gather | bytes 819200 | tf_op jit(solution)/shard_map/all_gather | solution.py:75
  99.3 4.9 %fusion.38 = f32[2,64,640]{2,1,0:T(8,128)S(1)} fusion(bf16[2,64,2560]{2,1,0:T(8,128)(2,1)S(1)} %all_gather.37, bf16[2,640,2560]{2,1,0:T(8,128)(2,1)} %param.10), kind=kOutput, calls=%fused_computation.68 | convolution fusion | flops 419430400 | bytes 7536640 | tf_op jit(solution)/shard_map/icb,irb->icr/dot_general | solution.py:73
  104.5 14.1 %all-gather.3 = f32[8,64,128]{2,1,0:T(8,128)S(1)} all-gather(f32[2,64,128]{2,1,0:T(8,128)S(1)} %fusion.22), channel_id=5, replica_groups=mesh['chain'=8,'col'=4] {'col'}, dimensions={0}, use_global_device_ids=true | all-gather | bytes 327680 | tf_op jit(solution)/shard_map/all_gather | solution.py:85
  119.0 9.4 %all-gather.4 = f32[512,128]{1,0:T(8,128)S(1)} all-gather(f32[64,128]{1,0:T(8,128)S(1)} %convolution_add_fusion.1), channel_id=6, replica_groups=mesh['chain'=8,'col'=4] {'chain'}, dimensions={0}, use_global_device_ids=true | all-gather | bytes 294912 | tf_op jit(solution)/shard_map/all_gather | solution.py:17
  128.6 10.2 %all-gather.2 = f32[1024,128]{1,0:T(8,128)S(1)} all-gather(f32[128,128]{1,0:T(8,128)S(1)} %convolution_select_fusion), channel_id=4, replica_groups=mesh['chain'=8,'col'=4] {'chain'}, dimensions={0}, use_global_device_ids=true | all-gather | bytes 589824 | tf_op jit(solution)/shard_map/all_gather | solution.py:17
  138.8 1.6 %while.27 = (s32[]{:T(128)}, f32[64,128]{1,0:T(8,128)S(1)}, s32[]{:T(128)}, f32[8,128,128]{2,1,0:T(8,128)S(1)}, f32[8,64,128]{2,1,0:T(8,128)S(1)}, /*index=5*/s32[]{:T(128)}, s32[]{:T(128)}, s32[]{:T(128)}, s32[]{:T(128)}) while((s32[]{:T(128)}, f32[64,128]{1,0:T(8,128)S(1)}, s32[]{:T(128)}, f32[8,128,128]{2,1,0:T(8,128)S(1)}, ...), condition=%wide.region_7.8_spmd, body=%wide.region_6.7_spmd.sunk | while | flops 12591110 | bytes 230539 | solution.py:26
  141.1 0.8 pad_maximum_fusion.1
  (42 shorter events, 3.8 us)
Async XLA Ops:
  6.5 8.2 %copy-start = (bf16[64,640]{1,0:T(8,128)(2,1)S(1)}, bf16[64,640]{1,0:T(8,128)(2,1)}, u32[]{:S(2)}) copy-start(bf16[64,640]{1,0:T(8,128)(2,1)} %param.13) | copy-start | bytes 245764
  6.5 72.6 %copy-start.4 = (bf16[2,64,640]{2,1,0:T(8,128)(2,1)S(1)}, bf16[2,64,640]{2,1,0:T(8,128)(2,1)}, u32[]{:S(2)}) copy-start(bf16[2,64,640]{2,1,0:T(8,128)(2,1)} %param.9) | copy-start | bytes 491524
  6.5 72.6 %copy-start.2 = (bf16[2,640,128]{2,1,0:T(8,128)(2,1)S(1)}, bf16[2,640,128]{2,1,0:T(8,128)(2,1)}, u32[]{:S(2)}) copy-start(bf16[2,640,128]{2,1,0:T(8,128)(2,1)} %param.11) | copy-start | bytes 983044
  6.5 48.9 %all-reduce.3.cloned.1.call-start = ((), (), s32[]{:S(2)}) async-start(), calls=%async_computation | async-start | bytes 393216 | tf_op jit(solution)/shard_map/psum | solution.py:51
  7.8 3.3 %collective-permute-start = (bf16[1,640,128]{1,2,0:T(8,128)(2,1)S(1)}, bf16[1,640,128]{1,2,0:T(8,128)(2,1)S(1)}, u32[]{:S(2)}, u32[]{:S(2)}) collective-permute-start(bf16[1,640,128]{1,2,0:T(8,128)(2,1)S(1)} %copy.13), channel_id=1, source_target_pairs={{4,0},{8,4},{12,8},{16,12},{20,16},{24,20},{28,24},{5,1},{9,5},{13... | collective-permute-start | bytes 491528 | tf_op jit(solution)/shard_map/ppermute | solution.py:10
  69.2 49.3 %copy-start.1 = (f32[2,128,128]{1,2,0:T(8,128)S(1)}, f32[2,128,128]{1,2,0:T(8,128)}, u32[]{:S(2)}) copy-start(f32[2,128,128]{1,2,0:T(8,128)} %get-tuple-element.155) | copy-start | bytes 393220
  82.0 58.6 %copy-start.3 = (bf16[2,640,128]{2,1,0:T(8,128)(2,1)S(1)}, bf16[2,640,128]{2,1,0:T(8,128)(2,1)}, u32[]{:S(2)}) copy-start(bf16[2,640,128]{2,1,0:T(8,128)(2,1)} %param.12) | copy-start | bytes 983044
Sparse Core Ops, SparseCore 0:
  14.9 40.5 all-reduce.2
